TPU v7x, 512 devices: a whole 4x8x8 slice. The times are simulated.
512 devices in a mesh: tile: 128 (over y, z, core), col: 4 (over x).
Axes of the slice: x: 4, y: 8, z: 8, core: 2. Of those that a mesh axis runs over, the one named last changes fastest.
Arguments:
- positions: float32 [3, 65536], P(None, 'tile'), may hold values from 0 to 10240, as said below
- trial_block: float32 [3, 16, 65536], P(None, None, 'tile')
- pair_tiles: int32 [2, 128, 4, 8], P(None, 'tile'), may hold values from 0 to 511, as said below
- pair_count: int32 [128, 4], P('tile'), may hold values from 0 to 8, as said below
Outputs:
- next_block: float32 [3, 16, 65536], P(None, None, 'tile')
- rayleigh: float32 [16, 16], replicated
- correlation_norm: float32 [16, 16], replicated
- residual_norms: float32 [16], replicated
Inputs may be any that keep to these rules, and one draw needn't show every extreme that they name: `positions`: tiles follow one another along the first component, in order of their numbers. `pair_tiles`: entry 1 lies between the row tile and two tiles past it, never below it, within the tiles of the same index along tile or of the next one. Each unordered pair of tiles is listed at most once among live slots; every pair of beads closer than 15 is covered by a live slot. Slots at or past the count hold valid numbers too. `pair_count`: for every index along tile but the last, one of its 4 devices along col has all 8 slots live.
All inputs are finite; a program needn't handle non-finite values.
Results may differ from a plain program's by a relative error of at most 0.0003.
Values sent between devices are 32-bit elements; how exact they have to be, the bound alone decides.
A program may use at most 64 MiB of HBM per device.

v0:
```python
import functools

import jax
import jax.numpy as jnp
from jax import lax
from jax.experimental import pallas as pl
from jax.experimental.pallas import tpu as pltpu
from jax.sharding import Mesh
from jax.sharding import PartitionSpec as P

TILE = ("ty", "tz", "core")
MESH = pl.DeviceIdType.MESH
F32 = jnp.float32
BF16 = jnp.bfloat16
HIGHEST = lax.Precision.HIGHEST

STEP = 0.2
MATS = ((0, 0), (0, 1), (0, 2), (1, 1), (1, 2), (2, 2))
MAT_OF = {(0, 0): 0, (0, 1): 1, (1, 0): 1, (0, 2): 2, (2, 0): 2, (1, 1): 3, (1, 2): 4, (2, 1): 4, (2, 2): 5}


def iota(shape, axis):
    return lax.broadcasted_iota(jnp.int32, shape, axis)


def split(x):
    hi = x.astype(BF16)
    return hi, (x - hi.astype(F32)).astype(BF16)


def mm(a, b):
    return lax.dot_general(a, b, (((1,), (0,)), ((), ())), preferred_element_type=F32)


def solve(z):
    m = z[:, 0:16]
    lane = iota((32, 16), 1)
    for j in range(16):
        col = m[:, j : j + 1]
        inv = 1.0 / m[j : j + 1, j : j + 1]
        row = m[j : j + 1, :] * inv
        m = jnp.where(lane == j, col * inv, m - col * row)
    return m[16:32, :]


def kernel(
    ny, nz, scale,
    x_ref, pos_ref, pairs_ref, count_ref,
    next_ref, ray_ref, corr_ref, norm_ref,
    xg, x1, pg, shi, slo, lw, dacc, pay, ra, rb, rc, tot,
    halo_send, halo_recv, p_send, p_recv, a_send, a_recv, b_send, b_recv, c_send, c_recv, t_send, t_recv,
):
    ty, tz, core, col = (lax.axis_index(n) for n in ("ty", "tz", "core", "col"))
    tiles = ny * nz * 2
    t = (ty * nz + tz) * 2 + core
    low = col < 2

    def at_tile(index, c):
        return (lax.div(index, 2 * nz), lax.rem(lax.div(index, 2), nz), lax.rem(index, 2), c)

    after, before = lax.rem(t + 1, tiles), lax.rem(t + tiles - 1, tiles)
    across = jnp.where(low, before, after)
    across_cols = (jnp.where(low, 2, 0), jnp.where(low, 3, 1))

    barrier = pltpu.get_barrier_semaphore()

    def greet(where):
        pl.semaphore_signal(barrier, inc=1, device_id=where, device_id_type=MESH)

    @pl.when(core == 1)
    def _():
        for o in range(1, ny):
            greet((lax.rem(ty + o, ny), tz, core, col))
        for o in range(1, nz):
            greet((ty, lax.rem(tz + o, nz), core, col))

    for c in across_cols:
        greet(at_tile(across, c))
    greet(at_tile(after, col))
    greet(at_tile(before, col))
    for o in range(1, 4):
        greet((ty, tz, core, lax.rem(col + o, 4)))
        greet((ty, tz, 1 - core, lax.rem(col + o, 4)))
    greet((ty, tz, 1 - core, col))

    lane = iota((1, 128), 1)
    rows, cols = pairs_ref[0], pairs_ref[1]
    slot_col = iota((4, 8), 0)
    counts = jnp.zeros((4, 8), jnp.int32)
    for c in range(4):
        counts = jnp.where(slot_col == c, count_ref[0, c], counts)
    live = jnp.where(iota((4, 8), 1) < counts, 1.0, 0.0).astype(F32)
    reach = cols - t * 4 - rows
    for r in range(4):
        xg[2 + r, 0:48, :] = x_ref[:, r * 128 : (r + 1) * 128]
        xg[2 + r, 48:56, :] = jnp.zeros((8, 128), F32)
        xg[2 + r, 48:51, :] = pos_ref[:, r * 128 : (r + 1) * 128]
        listed = jnp.zeros((1, 128), F32)
        for k in range(3):
            here = jnp.where((rows == r) & (reach == k), live, 0.0)
            total = jnp.sum(jnp.sum(here, axis=1, keepdims=True), axis=0, keepdims=True)
            listed = jnp.where(lane == k, total, listed)
        xg[2 + r, 51:52, :] = listed

    dacc[...] = jnp.zeros_like(dacc)
    own = 2 + col

    def spring_block(q, slot):
        mine = [xg[own, 48 + d : 49 + d, :] for d in range(3)]
        listed = xg[jnp.minimum(slot, own), 51:52, :]
        times = jnp.sum(jnp.where(lane == jnp.abs(slot - own), listed, 0.0), axis=1, keepdims=True)
        times = times * (1.0 / 64.0)
        near = jnp.transpose(xg[slot, 48:56, :])
        sums = [dacc[m] for m in range(6)]
        for ch in range(4):
            part = near[ch * 32 : (ch + 1) * 32]
            off = [part[:, d : d + 1] - mine[d] for d in range(3)]
            dist = off[0] * off[0] + off[1] * off[1] + off[2] * off[2]
            fall = 1.0 - dist * (1.0 / 225.0)
            weight = jnp.where(dist < 225.0, fall * fall, 0.0) * times / jnp.maximum(dist, 1.0)
            by = [weight * o for o in off]
            at = pl.ds(pl.multiple_of(q * 128 + ch * 32, 32), 32)
            for m, (c, d) in enumerate(MATS):
                s = by[c] * off[d]
                hi, lo = split(s)
                shi[at, m * 128 : (m + 1) * 128] = hi
                slo[at, m * 128 : (m + 1) * 128] = lo
                sums[m] = sums[m] + ((s[0:8] + s[8:16]) + (s[16:24] + s[24:32]))
        for m in range(6):
            dacc[m] = sums[m]

    first = jnp.where(low, 2, 3)
    late = (
        jnp.where(col == 0, 0, jnp.where(col == 1, 1, jnp.where(col == 2, 2, 6))),
        jnp.where(col == 0, 1, jnp.where(col == 1, 5, jnp.where(col == 2, 6, 7))),
    )
    slots = (first, first + 1, first + 2) + late

    pl.semaphore_wait(barrier, 11 + core * (ny + nz - 2))
    from_slot, to_slot = jnp.where(low, 4, 2), jnp.where(low, 0, 6)
    halo = pltpu.make_async_remote_copy(
        src_ref=xg.at[pl.ds(from_slot, 2)],
        dst_ref=xg.at[pl.ds(to_slot, 2)],
        send_sem=halo_send,
        recv_sem=halo_recv,
        device_id=at_tile(jnp.where(low, after, before), col),
        device_id_type=MESH,
    )
    halo.start()

    def near_vectors(source, q):
        hi, lo = split(source[slots[q], 0:48, :])
        lw[0:48, q * 128 : (q + 1) * 128] = hi
        lw[48:96, q * 128 : (q + 1) * 128] = lo

    def near_sum(start, stop):
        a, b = start * 128, stop * 128
        both = mm(lw[:, a:b], shi[a:b, :])
        return both[0:48] + both[48:96] + mm(lw[0:48, a:b], slo[a:b, :])

    def first_blocks(q, carry):
        spring_block(q, first + q)
        return carry

    lax.fori_loop(0, 3, first_blocks, 0)
    for q in range(3):
        near_vectors(xg, q)
    gathered = near_sum(0, 3)
    halo.wait_recv()

    def late_blocks(q, carry):
        spring_block(3 + q, jnp.where(q == 0, late[0], late[1]))
        return carry

    lax.fori_loop(0, 2, late_blocks, 0)
    for q in range(3, 5):
        near_vectors(xg, q)
    gathered = gathered + near_sum(3, 5)
    diag = [jnp.sum(dacc[m], axis=0, keepdims=True) for m in range(6)]

    def finish_product(gathered, source):
        here = [source[own, d * 16 : (d + 1) * 16, :] for d in range(3)]
        out = []
        for c in range(3):
            acc = None
            for d in range(3):
                m = MAT_OF[(c, d)]
                term = diag[m] * here[d] - gathered[d * 16 : (d + 1) * 16, m * 128 : (m + 1) * 128]
                acc = term if acc is None else acc + term
            out.append(acc)
        return here, out

    def exchange(it, here, product, halo_too):
        for d in range(3):
            pg[it, own, d * 16 : (d + 1) * 16, :] = product[d]
        both = jnp.concatenate([jnp.concatenate(here, axis=1), jnp.concatenate(product, axis=1)], axis=0)
        z = lax.dot_general(both, both, (((1,), (1,)), ((), ())), precision=HIGHEST, preferred_element_type=F32)
        for g in range(4):
            pay[it, :, g * 32 : (g + 1) * 32] = z[g * 8 : (g + 1) * 8, :]
        line = col * 2 + core

        def to_line(x):
            return pltpu.make_async_remote_copy(
                src_ref=pay.at[it], dst_ref=ra.at[it, line], send_sem=a_send.at[it, x], recv_sem=a_recv.at[it, line],
                device_id=(ty, tz, 1, x), device_id_type=MESH,
            )

        for x in range(4):
            @pl.when(jnp.logical_or(core == 0, col != x))
            def _():
                to_line(x).start()

        sent = []

        def send_product(n, slot, where):
            copy = pltpu.make_async_remote_copy(
                src_ref=pg.at[it, own], dst_ref=pg.at[it, slot], send_sem=p_send.at[it, n], recv_sem=p_recv.at[it, slot],
                device_id=where, device_id_type=MESH,
            )
            copy.start()
            sent.append(copy)

        if halo_too:
            for n, c in enumerate(across_cols):
                send_product(n, jnp.where(low, 6 + col, col - 2), at_tile(across, c))
        for o in range(1, 4):
            send_product(1 + o, own, (ty, tz, core, lax.rem(col + o, 4)))

        def summed(buf, n):
            acc = buf[it, 0]
            for i in range(1, n):
                acc = acc + buf[it, i]
            return acc

        @pl.when(core == 1)
        def _():
            ra[it, line] = pay[it]
            for o in range(1, 8):
                other = lax.rem(line + o, 8)
                pltpu.make_async_remote_copy(
                    src_ref=pay.at[it], dst_ref=ra.at[it, other], send_sem=a_send.at[it, 0],
                    recv_sem=a_recv.at[it, other], device_id=(ty, tz, 1, col), device_id_type=MESH,
                ).wait_recv()
            rb[it, ty] = summed(ra, 8)

            def along(buf, me, n, send, recv, place):
                copies = []
                for o in sorted(range(1, n), key=lambda o: -min(o, n - o)):
                    copy = pltpu.make_async_remote_copy(
                        src_ref=buf.at[it, me], dst_ref=buf.at[it, me], send_sem=send.at[it, o], recv_sem=recv.at[it, me],
                        device_id=place(lax.rem(me + o, n)), device_id_type=MESH,
                    )
                    copy.start()
                    copies.append(copy)
                for o in range(1, n):
                    other = lax.rem(me + o, n)
                    pltpu.make_async_remote_copy(
                        src_ref=buf.at[it, other], dst_ref=buf.at[it, other], send_sem=send.at[it, o],
                        recv_sem=recv.at[it, other], device_id=place(other), device_id_type=MESH,
                    ).wait_recv()
                return copies

            done = along(rb, ty, ny, b_send, b_recv, lambda i: (i, tz, 1, col))
            rc[it, tz] = summed(rb, ny)
            done += along(rc, tz, nz, c_send, c_recv, lambda i: (ty, i, 1, col))
            tot[it] = summed(rc, nz)
            down = pltpu.make_async_remote_copy(
                src_ref=tot.at[it], dst_ref=tot.at[it], send_sem=t_send.at[it], recv_sem=t_recv.at[it],
                device_id=(ty, tz, 0, col), device_id_type=MESH,
            )
            down.start()
            for copy in done:
                copy.wait_send()
            down.wait_send()

        @pl.when(core == 0)
        def _():
            pltpu.make_async_remote_copy(
                src_ref=tot.at[it], dst_ref=tot.at[it], send_sem=t_send.at[it], recv_sem=t_recv.at[it],
                device_id=(ty, tz, 1, col), device_id_type=MESH,
            ).wait_recv()

        def arrived(slot):
            pltpu.make_async_remote_copy(
                src_ref=pg.at[it, slot], dst_ref=pg.at[it, slot], send_sem=p_send.at[it, 0], recv_sem=p_recv.at[it, slot],
                device_id=(ty, tz, core, lax.rem(col + 1, 4)), device_id_type=MESH,
            ).wait_recv()

        for o in range(1, 4):
            arrived(2 + lax.rem(col + o, 4))
        if halo_too:
            for n in range(2):
                arrived(jnp.where(low, n, 6 + n))
        for copy in sent:
            copy.wait_send()
        for x in range(4):
            @pl.when(jnp.logical_or(core == 0, col != x))
            def _():
                to_line(x).wait_send()

        return jnp.concatenate([tot[it, :, g * 32 : (g + 1) * 32] for g in range(4)], axis=0)

    def updated(it, source, slot, c_hi, c_lo):
        out = []
        for d in range(3):
            x = source[slot, d * 16 : (d + 1) * 16, :]
            hi, lo = split(x)
            kept = mm(c_hi, hi) + mm(c_lo, hi) + mm(c_hi, lo)
            out.append(x - STEP * (pg[it, slot, d * 16 : (d + 1) * 16, :] - kept))
        return out

    here, product = finish_product(gathered, xg)
    z = exchange(0, here, product, True)
    c_hi, c_lo = split(solve(z))
    for i in range(6):
        slot = jnp.where(low, 0, 2) + i
        for d, part in enumerate(updated(0, xg, slot, c_hi, c_lo)):
            x1[slot, d * 16 : (d + 1) * 16, :] = part

    for q in range(5):
        near_vectors(x1, q)
    here, product = finish_product(near_sum(0, 5), x1)
    z = exchange(1, here, product, False)
    coef = solve(z)
    c_hi, c_lo = split(coef)
    for r in range(4):
        for d, part in enumerate(updated(1, x1, 2 + r, c_hi, c_lo)):
            next_ref[d * 16 : (d + 1) * 16, r * 128 : (r + 1) * 128] = part

    corr_ref[...] = z[0:16, 0:16] * scale
    ray_ref[...] = z[0:16, 16:32] * scale
    row = iota((16, 32), 0)
    squares = jnp.sum(jnp.where(iota((16, 32), 1) == row + 16, z[16:32, :], 0.0), axis=1, keepdims=True)
    norms = squares - jnp.sum(z[16:32, 0:16] * coef, axis=1, keepdims=True)
    square = (16, 16)
    norm_ref[...] = jnp.sum(jnp.where(iota(square, 0) == iota(square, 1), norms * scale, 0.0), axis=0, keepdims=True)
    halo.wait_send()


def per_device(ny, nz, positions, trial_block, pair_tiles, pair_count):
    scale = 1.0 / (3.0 * ny * nz * 2 * 512)
    vmem = pl.BlockSpec(memory_space=pltpu.VMEM)
    dma = pltpu.SemaphoreType.DMA
    n = max(ny, nz, 8)
    out = pl.pallas_call(
        functools.partial(kernel, ny, nz, scale),
        out_shape=(
            jax.ShapeDtypeStruct((48, 512), F32),
            jax.ShapeDtypeStruct((16, 16), F32),
            jax.ShapeDtypeStruct((16, 16), F32),
            jax.ShapeDtypeStruct((1, 16), F32),
        ),
        in_specs=[vmem, vmem, vmem, pl.BlockSpec(memory_space=pltpu.SMEM)],
        out_specs=(vmem, vmem, vmem, vmem),
        scratch_shapes=[
            pltpu.VMEM((8, 56, 128), F32),
            pltpu.VMEM((8, 48, 128), F32),
            pltpu.VMEM((2, 8, 48, 128), F32),
            pltpu.VMEM((640, 768), BF16),
            pltpu.VMEM((640, 768), BF16),
            pltpu.VMEM((96, 640), BF16),
            pltpu.VMEM((6, 8, 128), F32),
            pltpu.VMEM((2, 8, 128), F32),
            pltpu.VMEM((2, 8, 8, 128), F32),
            pltpu.VMEM((2, ny, 8, 128), F32),
            pltpu.VMEM((2, nz, 8, 128), F32),
            pltpu.VMEM((2, 8, 128), F32),
            dma, dma,
            dma((2, 8)), dma((2, 8)),
            dma((2, 4)), dma((2, 8)),
            dma((2, n)), dma((2, n)),
            dma((2, n)), dma((2, n)),
            dma((2,)), dma((2,)),
        ],
        compiler_params=pltpu.CompilerParams(collective_id=0, has_side_effects=True),
        name="block_step",
    )(trial_block.reshape(48, 512), positions, pair_tiles.reshape(2, 4, 8), pair_count)
    block, rayleigh, correlation, norms = out
    return block.reshape(3, 16, 512), rayleigh, correlation, norms.reshape(16)


def build(finer):
    return jax.shard_map(
        functools.partial(per_device, finer.shape["ty"], finer.shape["tz"]),
        mesh=finer,
        in_specs=(P(None, TILE), P(None, None, TILE), P(None, TILE, None, None), P(TILE, None)),
        out_specs=(P(None, None, TILE), P(), P(), P()),
        check_vma=False,
    )


def solution(mesh):
    return build(Mesh(mesh.devices.reshape(8, 8, 2, mesh.shape["col"]), (*TILE, "col")))
```

profile of v0, /device:TPU:1, one launch (start us, length us, event | category | flops | bytes accessed | tf_op | source)
XLA Modules:
  0.0 53.3 jit_solution(10301685232870727491)
XLA Ops:
  0.6 49.2 %block_step.1 = (f32[48,512]{1,0:T(8,128)}, f32[16,16]{1,0:T(8,128)}, f32[16,16]{1,0:T(8,128)}, f32[1,16]{1,0:T(1,128)}) custom-call(f32[48,512]{1,0:T(8,128)} %bitcast.4, f32[3,512]{1,0:T(4,128)} %pos_ref.1, s32[2,4,8]{2,1,0:T(4,128)} %bitcast.6, s32[1,4]{1,0:T(1,128)} %count_ref.1), custom_call_target="tpu_custom_call" | custom-call | tf_op jit(solution)/shard_map/block_step/pallas_call | solution.py:345
  49.9 0.0 copy-start.1
  49.9 1.5 %copy.12 = f32[3,16,512]{2,1,0:T(8,128)} copy(f32[3,16,512]{2,1,0:T(8,128)} %bitcast.5) | data formatting | bytes 196608
  51.4 0.0 copy-done.1
  51.4 0.0 copy-start
  51.4 0.6 %copy.13 = f32[16,16]{1,0:T(8,128)} copy(f32[16,16]{1,0:T(8,128)S(1)} %copy-done.1) | data formatting | bytes 2048
  52.0 0.1 copy-done
  52.1 0.0 copy-start.2
  52.2 0.6 %copy.14 = f32[16,16]{1,0:T(8,128)} copy(f32[16,16]{1,0:T(8,128)S(1)} %copy-done) | data formatting | bytes 2048
  52.7 0.1 copy-done.2
  52.8 0.5 copy.15
Async XLA Ops:
  49.9 1.6 %copy-start.1 = (f32[16,16]{1,0:T(8,128)S(1)}, f32[16,16]{1,0:T(8,128)}, u32[]{:S(2)}) copy-start(f32[16,16]{1,0:T(8,128)} %get-tuple-element.17) | copy-start | bytes 3076
  51.4 0.7 %copy-start = (f32[16,16]{1,0:T(8,128)S(1)}, f32[16,16]{1,0:T(8,128)}, u32[]{:S(2)}) copy-start(f32[16,16]{1,0:T(8,128)} %get-tuple-element.18) | copy-start | bytes 3076
  52.1 0.7 %copy-start.2 = (f32[1,16]{1,0:T(1,128)S(1)}, f32[1,16]{1,0:T(1,128)}, u32[]{:S(2)}) copy-start(f32[1,16]{1,0:T(1,128)} %get-tuple-element.11) | copy-start | bytes 196
where the time goes:
time: 53.6 us; the launch traced here: 53.3 us
  Pallas kernels  49.2 us (92%)
  local copies, waits for them, and re-layouts  3.43 us (6%)
  between operations  0.65 us (1%)
    pallas_call x1, Pallas kernels, per_device(): pl.pallas_call(functools.partial(kernel, ny, nz, scale), out_shape=(jax.S...  49.2 us
    unnamed x10, local copies, waits for them, and re-layouts  3.43 us

commit v1 on v0

v1 whole, which is shorter than its diff:
```python
import functools

import jax
import jax.numpy as jnp
from jax import lax
from jax.experimental import pallas as pl
from jax.experimental.pallas import tpu as pltpu
from jax.sharding import Mesh
from jax.sharding import PartitionSpec as P

TILE = ("ty", "tz", "core")
MESH = pl.DeviceIdType.MESH
F32 = jnp.float32
BF16 = jnp.bfloat16
HIGHEST = lax.Precision.HIGHEST

STEP = 0.2
MATS = ((0, 0), (0, 1), (0, 2), (1, 1), (1, 2), (2, 2))
MAT_OF = {(0, 0): 0, (0, 1): 1, (1, 0): 1, (0, 2): 2, (2, 0): 2, (1, 1): 3, (1, 2): 4, (2, 1): 4, (2, 2): 5}


def iota(shape, axis):
    return lax.broadcasted_iota(jnp.int32, shape, axis)


def split(x):
    hi = x.astype(BF16)
    return hi, (x - hi.astype(F32)).astype(BF16)


def mm(a, b):
    return lax.dot_general(a, b, (((1,), (0,)), ((), ())), preferred_element_type=F32)


def mm_exact(a, b, transposed=False):
    dims = (((1,), (1 if transposed else 0,)), ((), ()))
    return lax.dot_general(a, b, dims, precision=HIGHEST, preferred_element_type=F32)


def solve(corr, gram):
    m = jnp.concatenate([corr, gram], axis=0)
    lane = iota((32, 16), 1)
    for j in range(16):
        col = m[:, j : j + 1]
        inv = 1.0 / m[j : j + 1, j : j + 1]
        row = m[j : j + 1, :] * inv
        m = jnp.where(lane == j, col * inv, m - col * row)
    return m[16:32, :]


def finish(scale, xpq_ref, z_ref, next_ref, ray_ref, corr_ref, norm_ref):
    xx, xp, pp, pq = (z_ref[:, 16 * i : 16 * i + 16] for i in range(4))
    qq = z_ref[:, 64:65]
    eye = iota((16, 16), 0) == iota((16, 16), 1)
    one = jnp.where(eye, 1.0, 0.0).astype(F32)
    c0 = solve(xx, xp)
    at = one + STEP * c0
    left = mm_exact(at, jnp.concatenate([xx, xp, pp, pq], axis=1))
    a_xx, a_xp, a_pp, a_pq = (left[:, 16 * i : 16 * i + 16] for i in range(4))
    y1, y2, y3 = a_xx - STEP * xp, a_xp - STEP * pp, a_pp - STEP * pq
    right = mm_exact(jnp.concatenate([y1, y2], axis=0), at, transposed=True)
    corr = right[0:16] - STEP * y2
    gram = right[16:32] - STEP * y3
    c1 = solve(corr, gram)

    both = c0 + c1
    factor = jnp.concatenate([STEP * both + STEP * STEP * mm_exact(c1, c0), -STEP * STEP * both], axis=1)
    f_hi, f_lo = split(factor)
    for r in range(4):
        for d in range(3):
            rows, lanes = slice(d * 16, (d + 1) * 16), slice(r * 128, (r + 1) * 128)
            x, p, q = (xpq_ref[i, r, rows, :] for i in range(3))
            hi, lo = split(jnp.concatenate([x, p], axis=0))
            moved = mm(f_hi, hi) + mm(f_lo, hi) + mm(f_hi, lo)
            next_ref[rows, lanes] = (x - 2.0 * STEP * p) + (moved + STEP * STEP * q)

    corr_ref[...] = corr * scale
    ray_ref[...] = gram * scale
    squares = jnp.sum(a_pp * at - 2.0 * STEP * jnp.where(eye, a_pq, 0.0), axis=1, keepdims=True) + STEP * STEP * qq
    norms = (squares - jnp.sum(gram * c1, axis=1, keepdims=True)) * scale
    norm_ref[...] = jnp.sum(jnp.where(eye, norms, 0.0), axis=0, keepdims=True)


def kernel(
    ny, nz,
    x_hbm, pos_hbm, pairs_hbm, count_hbm,
    xpq_ref, z_ref,
    pos_ref, pairs_ref, count_ref, in_sem,
    xg, pg, qg, shi, slo, lw, dacc, pay, ra, rb, rc,
    halo_send, halo_recv, p_send, p_recv, q_send, q_recv, a_send, a_recv, b_send, b_recv, c_send, c_recv,
):
    ty, tz, core, col = (lax.axis_index(n) for n in ("ty", "tz", "core", "col"))
    tiles = ny * nz * 2
    t = (ty * nz + tz) * 2 + core
    low = col < 2

    def at_tile(index, c):
        return (lax.div(index, 2 * nz), lax.rem(lax.div(index, 2), nz), lax.rem(index, 2), c)

    after, before = lax.rem(t + 1, tiles), lax.rem(t + tiles - 1, tiles)
    across = jnp.where(low, before, after)
    across_cols = (jnp.where(low, 2, 0), jnp.where(low, 3, 1))

    fetches = [
        pltpu.make_async_copy(count_hbm, count_ref, in_sem.at[0]),
        pltpu.make_async_copy(pairs_hbm, pairs_ref, in_sem.at[1]),
        pltpu.make_async_copy(pos_hbm, pos_ref, in_sem.at[2]),
    ]
    for r in range(4):
        lanes = slice(r * 128, (r + 1) * 128)
        fetches.append(pltpu.make_async_copy(x_hbm.at[:, lanes], xg.at[2 + r, 0:48, :], in_sem.at[3 + r]))
    for fetch in fetches:
        fetch.start()

    barrier = pltpu.get_barrier_semaphore()

    def greet(where):
        pl.semaphore_signal(barrier, inc=1, device_id=where, device_id_type=MESH)

    @pl.when(core == 1)
    def _():
        for o in range(1, ny):
            greet((lax.rem(ty + o, ny), tz, core, col))
        for o in range(1, nz):
            greet((ty, lax.rem(tz + o, nz), core, col))

    @pl.when(core == 0)
    def _():
        for o in range(1, nz):
            greet((ty, lax.rem(tz + o, nz), 1, col))

    for c in across_cols:
        greet(at_tile(across, c))
    greet(at_tile(after, col))
    greet(at_tile(before, col))
    for o in range(1, 4):
        greet((ty, tz, core, lax.rem(col + o, 4)))
        greet((ty, tz, 1 - core, lax.rem(col + o, 4)))
    greet((ty, tz, 1 - core, col))

    for fetch in fetches:
        fetch.wait()
    lane = iota((1, 128), 1)
    rows, cols = pairs_ref[0], pairs_ref[1]
    slot_col = iota((4, 8), 0)
    counts = jnp.zeros((4, 8), jnp.int32)
    for c in range(4):
        counts = jnp.where(slot_col == c, count_ref[:, c : c + 1], counts)
    live = jnp.where(iota((4, 8), 1) < counts, 1.0, 0.0).astype(F32)
    reach = cols - t * 4 - rows
    for r in range(4):
        xg[2 + r, 48:56, :] = jnp.zeros((8, 128), F32)
        xg[2 + r, 48:51, :] = pos_ref[:, r * 128 : (r + 1) * 128]
        listed = jnp.zeros((1, 128), F32)
        for k in range(3):
            here = jnp.where((rows == r) & (reach == k), live, 0.0)
            total = jnp.sum(jnp.sum(here, axis=1, keepdims=True), axis=0, keepdims=True)
            listed = jnp.where(lane == k, total, listed)
        xg[2 + r, 51:52, :] = listed

    dacc[...] = jnp.zeros_like(dacc)
    own = 2 + col

    def spring_block(q, slot):
        mine = [xg[own, 48 + d : 49 + d, :] for d in range(3)]
        listed = xg[jnp.minimum(slot, own), 51:52, :]
        times = jnp.sum(jnp.where(lane == jnp.abs(slot - own), listed, 0.0), axis=1, keepdims=True)
        times = times * (1.0 / 64.0)
        near = jnp.transpose(xg[slot, 48:56, :])
        sums = [dacc[m] for m in range(6)]
        for ch in range(4):
            part = near[ch * 32 : (ch + 1) * 32]
            off = [part[:, d : d + 1] - mine[d] for d in range(3)]
            dist = off[0] * off[0] + off[1] * off[1] + off[2] * off[2]
            fall = 1.0 - dist * (1.0 / 225.0)
            weight = jnp.where(dist < 225.0, fall * fall, 0.0) * times / jnp.maximum(dist, 1.0)
            by = [weight * o for o in off]
            at = pl.ds(pl.multiple_of(q * 128 + ch * 32, 32), 32)
            for m, (c, d) in enumerate(MATS):
                s = by[c] * off[d]
                hi, lo = split(s)
                shi[at, m * 128 : (m + 1) * 128] = hi
                slo[at, m * 128 : (m + 1) * 128] = lo
                sums[m] = sums[m] + ((s[0:8] + s[8:16]) + (s[16:24] + s[24:32]))
        for m in range(6):
            dacc[m] = sums[m]

    first = jnp.where(low, 2, 3)
    late = (
        jnp.where(col == 0, 0, jnp.where(col == 1, 1, jnp.where(col == 2, 2, 6))),
        jnp.where(col == 0, 1, jnp.where(col == 1, 5, jnp.where(col == 2, 6, 7))),
    )
    slots = (first, first + 1, first + 2) + late

    pl.semaphore_wait(barrier, 11 + core * (ny + 2 * nz - 3))
    from_slot, to_slot = jnp.where(low, 4, 2), jnp.where(low, 0, 6)
    halo = pltpu.make_async_remote_copy(
        src_ref=xg.at[pl.ds(from_slot, 2)],
        dst_ref=xg.at[pl.ds(to_slot, 2)],
        send_sem=halo_send,
        recv_sem=halo_recv,
        device_id=at_tile(jnp.where(low, after, before), col),
        device_id_type=MESH,
    )
    halo.start()

    def near_vectors(source, q):
        hi, lo = split(source[slots[q], 0:48, :])
        lw[0:48, q * 128 : (q + 1) * 128] = hi
        lw[48:96, q * 128 : (q + 1) * 128] = lo

    def near_sum(start, stop):
        a, b = start * 128, stop * 128
        both = mm(lw[:, a:b], shi[a:b, :])
        return both[0:48] + both[48:96] + mm(lw[0:48, a:b], slo[a:b, :])

    def first_blocks(q, carry):
        spring_block(q, first + q)
        return carry

    lax.fori_loop(0, 3, first_blocks, 0)
    for q in range(3):
        near_vectors(xg, q)
    gathered = near_sum(0, 3)
    halo.wait_recv()

    def late_blocks(q, carry):
        spring_block(3 + q, jnp.where(q == 0, late[0], late[1]))
        return carry

    lax.fori_loop(0, 2, late_blocks, 0)
    for q in range(3, 5):
        near_vectors(xg, q)
    gathered = gathered + near_sum(3, 5)
    diag = [jnp.sum(dacc[m], axis=0, keepdims=True) for m in range(6)]

    def finish_product(gathered, source):
        here = [source[own, d * 16 : (d + 1) * 16, :] for d in range(3)]
        out = []
        for c in range(3):
            acc = None
            for d in range(3):
                m = MAT_OF[(c, d)]
                term = diag[m] * here[d] - gathered[d * 16 : (d + 1) * 16, m * 128 : (m + 1) * 128]
                acc = term if acc is None else acc + term
            out.append(acc)
        return here, out

    def moved(buf, at, send, recv, where):
        return pltpu.make_async_remote_copy(
            src_ref=buf.at[at], dst_ref=buf.at[at], send_sem=send, recv_sem=recv, device_id=where, device_id_type=MESH
        )

    here, first_product = finish_product(gathered, xg)
    for d in range(3):
        pg[own, d * 16 : (d + 1) * 16, :] = first_product[d]
    sent = []
    for n, c in enumerate(across_cols):
        sent.append(
            pltpu.make_async_remote_copy(
                src_ref=pg.at[own], dst_ref=pg.at[jnp.where(low, 6 + col, col - 2)], send_sem=p_send.at[n],
                recv_sem=p_recv.at[jnp.where(low, 6 + col, col - 2)], device_id=at_tile(across, c), device_id_type=MESH,
            )
        )
    for o in range(1, 4):
        sent.append(moved(pg, own, p_send.at[1 + o], p_recv.at[own], (ty, tz, core, lax.rem(col + o, 4))))
    for copy in sent:
        copy.start()

    def arrived(buf, slot, recv):
        moved(buf, slot, p_send.at[0], recv, (ty, tz, core, lax.rem(col + 1, 4))).wait_recv()

    for o in range(1, 4):
        other = 2 + lax.rem(col + o, 4)
        arrived(pg, other, p_recv.at[other])
    for n in range(2):
        other = jnp.where(low, n, 6 + n)
        arrived(pg, other, p_recv.at[other])

    for q in range(5):
        near_vectors(pg, q)
    _, second_product = finish_product(near_sum(0, 5), pg)

    for d in range(3):
        qg[col, d * 16 : (d + 1) * 16, :] = second_product[d]
    x, p, q = (jnp.concatenate(parts, axis=1) for parts in (here, first_product, second_product))
    z = mm_exact(jnp.concatenate([x, p], axis=0), jnp.concatenate([x, p, q], axis=0), transposed=True)
    pay[:, 0:32] = z[0:16, 0:32]
    pay[:, 32:64] = z[16:32, 16:48]
    pay[:, 64:128] = jnp.broadcast_to(jnp.sum(q * q, axis=1, keepdims=True), (16, 64))

    line = col * 2 + core

    def to_line(x):
        return pltpu.make_async_remote_copy(
            src_ref=pay, dst_ref=ra.at[line], send_sem=a_send.at[x], recv_sem=a_recv.at[line],
            device_id=(ty, tz, 1, x), device_id_type=MESH,
        )

    for x in range(4):
        @pl.when(jnp.logical_or(core == 0, col != x))
        def _():
            to_line(x).start()

    for o in range(1, 4):
        copy = moved(qg, col, q_send.at[o - 1], q_recv.at[col], (ty, tz, core, lax.rem(col + o, 4)))
        copy.start()
        sent.append(copy)

    def summed(buf, n):
        parts = [buf[i] for i in range(n)]
        while len(parts) > 1:
            parts = [a + b for a, b in zip(parts[0::2], parts[1::2])] + parts[len(parts) & ~1 :]
        return parts[0]

    def far_first(n):
        return sorted(range(1, n), key=lambda o: -min(o, n - o))

    @pl.when(core == 1)
    def _():
        ra[line] = pay[...]
        for o in range(1, 8):
            other = lax.rem(line + o, 8)
            moved(ra, other, a_send.at[0], a_recv.at[other], (ty, tz, 0, col)).wait_recv()
        rb[ty] = summed(ra, 8)
        done = []
        for o in far_first(ny):
            done.append(moved(rb, ty, b_send.at[o], b_recv.at[ty], (lax.rem(ty + o, ny), tz, 1, col)))
            done[-1].start()
        for o in range(1, ny):
            other = lax.rem(ty + o, ny)
            moved(rb, other, b_send.at[o], b_recv.at[other], (other, tz, 1, col)).wait_recv()
        rc[tz] = summed(rb, ny)
        for o in far_first(nz) + [0]:
            place = lax.rem(tz + o, nz)
            done.append(moved(rc, tz, c_send.at[0, o], c_recv.at[tz], (ty, place, 0, col)))
            done[-1].start()
            if o:
                done.append(moved(rc, tz, c_send.at[1, o], c_recv.at[tz], (ty, place, 1, col)))
                done[-1].start()
        for o in range(1, nz):
            other = lax.rem(tz + o, nz)
            moved(rc, other, c_send.at[0, 0], c_recv.at[other], (ty, tz, 0, col)).wait_recv()
        for copy in done:
            copy.wait_send()

    @pl.when(core == 0)
    def _():
        for other in range(nz):
            moved(rc, other, c_send.at[0, 0], c_recv.at[other], (ty, tz, 1, col)).wait_recv()

    z_ref[...] = summed(rc, nz)
    for o in range(1, 4):
        other = lax.rem(col + o, 4)
        arrived(qg, other, q_recv.at[other])
    for r in range(4):
        xpq_ref[0, r] = xg[2 + r, 0:48, :]
        xpq_ref[1, r] = pg[2 + r]
        xpq_ref[2, r] = qg[r]
    for copy in sent:
        copy.wait_send()
    for x in range(4):
        @pl.when(jnp.logical_or(core == 0, col != x))
        def _():
            to_line(x).wait_send()
    halo.wait_send()


def per_device(ny, nz, positions, trial_block, pair_tiles, pair_count):
    scale = 1.0 / (3.0 * ny * nz * 2 * 512)
    vmem = pl.BlockSpec(memory_space=pltpu.VMEM)
    dma = pltpu.SemaphoreType.DMA
    hbm = pl.BlockSpec(memory_space=pltpu.HBM)
    products, gram = pl.pallas_call(
        functools.partial(kernel, ny, nz),
        out_shape=(jax.ShapeDtypeStruct((3, 4, 48, 128), F32), jax.ShapeDtypeStruct((16, 128), F32)),
        in_specs=[hbm] * 4,
        out_specs=(vmem, vmem),
        scratch_shapes=[
            pltpu.VMEM((3, 512), F32),
            pltpu.VMEM((2, 4, 8), jnp.int32),
            pltpu.VMEM((1, 4), jnp.int32),
            dma((7,)),
            pltpu.VMEM((8, 56, 128), F32),
            pltpu.VMEM((8, 48, 128), F32),
            pltpu.VMEM((4, 48, 128), F32),
            pltpu.VMEM((640, 768), BF16),
            pltpu.VMEM((640, 768), BF16),
            pltpu.VMEM((96, 640), BF16),
            pltpu.VMEM((6, 8, 128), F32),
            pltpu.VMEM((16, 128), F32),
            pltpu.VMEM((8, 16, 128), F32),
            pltpu.VMEM((ny, 16, 128), F32),
            pltpu.VMEM((nz, 16, 128), F32),
            dma, dma,
            dma((5,)), dma((8,)),
            dma((3,)), dma((4,)),
            dma((4,)), dma((8,)),
            dma((ny,)), dma((ny,)),
            dma((2, nz)), dma((nz,)),
        ],
        compiler_params=pltpu.CompilerParams(collective_id=0, has_side_effects=True, vmem_limit_bytes=16 << 20),
        name="gram_blocks",
    )(trial_block.reshape(48, 512), positions, pair_tiles.reshape(2, 4, 8), pair_count)
    block, rayleigh, correlation, norms = pl.pallas_call(
        functools.partial(finish, scale),
        out_shape=(
            jax.ShapeDtypeStruct((48, 512), F32),
            jax.ShapeDtypeStruct((16, 16), F32),
            jax.ShapeDtypeStruct((16, 16), F32),
            jax.ShapeDtypeStruct((1, 16), F32),
        ),
        in_specs=[vmem] * 2,
        out_specs=(vmem,) * 4,
        compiler_params=pltpu.CompilerParams(vmem_limit_bytes=16 << 20),
        name="finish",
    )(products, gram)
    return block.reshape(3, 16, 512), rayleigh, correlation, norms.reshape(16)


def build(finer):
    return jax.shard_map(
        functools.partial(per_device, finer.shape["ty"], finer.shape["tz"]),
        mesh=finer,
        in_specs=(P(None, TILE), P(None, None, TILE), P(None, TILE, None, None), P(TILE, None)),
        out_specs=(P(None, None, TILE), P(), P(), P()),
        check_vma=False,
    )


def solution(mesh):
    return build(Mesh(mesh.devices.reshape(8, 8, 2, mesh.shape["col"]), (*TILE, "col")))
```

time: 53.6 us -> 44 us (0.82)
  Pallas kernels: 49.2 us -> 40.2 us
    pallas_call x1 -> x2, Pallas kernels: 49.2 us -> 40.2 us  [the longest x1 36.2 us: per_device(): pl.pallas_call(functools.partial(kernel, ny, nz), out_shape=(jax.ShapeDty...]
    unnamed x10 -> x8, local copies, waits for them, and re-layouts: 3.43 us -> 2.92 us
where the time goes in v1:
time: 44 us; the launch traced here: 43.8 us
  Pallas kernels  40.2 us (91%)
  local copies, waits for them, and re-layouts  2.92 us (7%)
  between operations  0.65 us (1%)
    pallas_call x1, Pallas kernels, per_device(): pl.pallas_call(functools.partial(kernel, ny, nz), out_shape=(jax.ShapeDty...  36.2 us
    pallas_call x1, Pallas kernels, per_device(): pl.pallas_call(functools.partial(finish, scale), out_shape=(jax.ShapeDtyp...  4.03 us
    unnamed x8, local copies, waits for them, and re-layouts  2.92 us

profile of v1, /device:TPU:1, one launch (start us, length us, event | category | flops | bytes accessed | tf_op | source)
XLA Modules:
  0.0 43.8 jit_solution(13493880957686008223)
XLA Ops:
  0.6 0.0 copy-start.3
  0.6 0.6 %copy-done.3 = s32[1,4]{1,0:T(1,128)S(1)} copy-done((s32[1,4]{1,0:T(1,128)S(1)}, s32[1,4]{1,0:T(1,128)}, u32[]{:S(2)}) %copy-start.3) | copy-done | bytes 40
  1.3 0.0 copy-start
  1.3 0.9 %copy-done = f32[3,16,512]{2,1,0:T(8,128)S(1)} copy-done((f32[3,16,512]{2,1,0:T(8,128)S(1)}, f32[3,16,512]{2,1,0:T(8,128)}, u32[]{:S(2)}) %copy-start) | copy-done | bytes 98328
  2.2 0.0 copy-start.1
  2.2 0.7 %copy-done.1 = f32[3,512]{1,0:T(4,128)S(1)} copy-done((f32[3,512]{1,0:T(4,128)S(1)}, f32[3,512]{1,0:T(4,128)}, u32[]{:S(2)}) %copy-start.1) | copy-done | bytes 6168
  2.9 0.0 copy-start.2
  2.9 0.7 %copy-done.2 = s32[2,1,4,8]{3,2,1,0:T(4,128)S(1)} copy-done((s32[2,1,4,8]{3,2,1,0:T(4,128)S(1)}, s32[2,1,4,8]{3,2,1,0:T(4,128)}, u32[]{:S(2)}) %copy-start.2) | copy-done | bytes 280
  3.6 36.2 %gram_blocks.1 = (f32[3,4,48,128]{3,2,1,0:T(8,128)S(1)}, f32[16,128]{1,0:T(8,128)S(1)}) custom-call(f32[48,512]{1,0:T(8,128)S(1)} %bitcast.4, f32[3,512]{1,0:T(4,128)S(1)} %copy-done.1, s32[2,4,8]{2,1,0:T(4,128)S(1)} %bitcast.5, s32[1,4]{1,0:T(1,128)S(1)} %copy-done.3), custom_call_target="tpu_custom_call" | custom-call | tf_op jit(solution)/shard_map/gram_blocks/pallas_call | solution.py:374
  39.8 4.0 %finish.1 = (f32[48,512]{1,0:T(8,128)}, f32[16,16]{1,0:T(8,128)}, f32[16,16]{1,0:T(8,128)}, f32[1,16]{1,0:T(1,128)}) custom-call(f32[3,4,48,128]{3,2,1,0:T(8,128)S(1)} %get-tuple-element.10.xpq_ref, f32[16,128]{1,0:T(8,128)S(1)} %get-tuple-element.11.z_ref), custom_call_target="tpu_custom_call" | custom-call | tf_op jit(solution)/shard_map/finish/pallas_call | solution.py:405
Async XLA Ops:
  0.6 0.7 %copy-start.3 = (s32[1,4]{1,0:T(1,128)S(1)}, s32[1,4]{1,0:T(1,128)}, u32[]{:S(2)}) copy-start(s32[1,4]{1,0:T(1,128)} %count_hbm.1) | copy-start | bytes 52
  1.3 0.9 %copy-start = (f32[3,16,512]{2,1,0:T(8,128)S(1)}, f32[3,16,512]{2,1,0:T(8,128)}, u32[]{:S(2)}) copy-start(f32[3,16,512]{2,1,0:T(8,128)} %param.5) | copy-start | bytes 294916
  2.2 0.7 %copy-start.1 = (f32[3,512]{1,0:T(4,128)S(1)}, f32[3,512]{1,0:T(4,128)}, u32[]{:S(2)}) copy-start(f32[3,512]{1,0:T(4,128)} %pos_hbm.1) | copy-start | bytes 18436
  2.9 0.7 %copy-start.2 = (s32[2,1,4,8]{3,2,1,0:T(4,128)S(1)}, s32[2,1,4,8]{3,2,1,0:T(4,128)}, u32[]{:S(2)}) copy-start(s32[2,1,4,8]{3,2,1,0:T(4,128)} %param.6) | copy-start | bytes 772

commit v2 on v1

--- a/solution.py
+++ b/solution.py
@@ -39,16 +39,24 @@
 
 def solve(corr, gram):
     m = jnp.concatenate([corr, gram], axis=0)
-    lane = iota((32, 16), 1)
+    shape = (32, 16)
+    lane = iota(shape, 1)
+    wide = [jnp.broadcast_to(m[:, j : j + 1], shape) for j in range(16)]
     for j in range(16):
-        col = m[:, j : j + 1]
-        inv = 1.0 / m[j : j + 1, j : j + 1]
-        row = m[j : j + 1, :] * inv
-        m = jnp.where(lane == j, col * inv, m - col * row)
+        col = wide[j] / jnp.broadcast_to(wide[j][j : j + 1, :], shape)
+        m = jnp.where(lane == j, col, m - col * jnp.broadcast_to(m[j : j + 1, :], shape))
+        for n in range(j + 1, 16):
+            wide[n] = wide[n] - col * jnp.broadcast_to(wide[n][j : j + 1, :], shape)
     return m[16:32, :]
 
 
-def finish(scale, xpq_ref, z_ref, next_ref, ray_ref, corr_ref, norm_ref):
+def finish(scale, x_hbm, pq_hbm, z_hbm, next_ref, ray_ref, corr_ref, norm_ref, x_ref, pq_ref, z_ref, in_sem):
+    gram_in = pltpu.make_async_copy(z_hbm, z_ref, in_sem.at[0])
+    x_in = pltpu.make_async_copy(x_hbm, x_ref, in_sem.at[1])
+    pq_in = pltpu.make_async_copy(pq_hbm, pq_ref, in_sem.at[2])
+    for copy in (gram_in, x_in, pq_in):
+        copy.start()
+    gram_in.wait()
     xx, xp, pp, pq = (z_ref[:, 16 * i : 16 * i + 16] for i in range(4))
     qq = z_ref[:, 64:65]
     eye = iota((16, 16), 0) == iota((16, 16), 1)
@@ -66,10 +74,12 @@
     both = c0 + c1
     factor = jnp.concatenate([STEP * both + STEP * STEP * mm_exact(c1, c0), -STEP * STEP * both], axis=1)
     f_hi, f_lo = split(factor)
+    x_in.wait()
+    pq_in.wait()
     for r in range(4):
         for d in range(3):
             rows, lanes = slice(d * 16, (d + 1) * 16), slice(r * 128, (r + 1) * 128)
-            x, p, q = (xpq_ref[i, r, rows, :] for i in range(3))
+            x, p, q = x_ref[rows, lanes], pq_ref[0, r, rows, :], pq_ref[1, r, rows, :]
             hi, lo = split(jnp.concatenate([x, p], axis=0))
             moved = mm(f_hi, hi) + mm(f_lo, hi) + mm(f_hi, lo)
             next_ref[rows, lanes] = (x - 2.0 * STEP * p) + (moved + STEP * STEP * q)
@@ -84,8 +94,8 @@
 def kernel(
     ny, nz,
     x_hbm, pos_hbm, pairs_hbm, count_hbm,
-    xpq_ref, z_ref,
-    pos_ref, pairs_ref, count_ref, in_sem,
+    pq_hbm, z_hbm,
+    pos_ref, pairs_ref, count_ref, in_sem, z_ref, out_sem,
     xg, pg, qg, shi, slo, lw, dacc, pay, ra, rb, rc,
     halo_send, halo_recv, p_send, p_recv, q_send, q_recv, a_send, a_recv, b_send, b_recv, c_send, c_recv,
 ):
@@ -316,6 +326,18 @@
     def far_first(n):
         return sorted(range(1, n), key=lambda o: -min(o, n - o))
 
+    products_out = (
+        pltpu.make_async_copy(pg.at[2:6], pq_hbm.at[0], out_sem.at[1]),
+        pltpu.make_async_copy(qg, pq_hbm.at[1], out_sem.at[2]),
+    )
+
+    def put_products():
+        for o in range(1, 4):
+            other = lax.rem(col + o, 4)
+            arrived(qg, other, q_recv.at[other])
+        for copy in products_out:
+            copy.start()
+
     @pl.when(core == 1)
     def _():
         ra[line] = pay[...]
@@ -327,6 +349,7 @@
         for o in far_first(ny):
             done.append(moved(rb, ty, b_send.at[o], b_recv.at[ty], (lax.rem(ty + o, ny), tz, 1, col)))
             done[-1].start()
+        put_products()
         for o in range(1, ny):
             other = lax.rem(ty + o, ny)
             moved(rb, other, b_send.at[o], b_recv.at[other], (other, tz, 1, col)).wait_recv()
@@ -346,17 +369,13 @@
 
     @pl.when(core == 0)
     def _():
+        put_products()
         for other in range(nz):
             moved(rc, other, c_send.at[0, 0], c_recv.at[other], (ty, tz, 1, col)).wait_recv()
 
     z_ref[...] = summed(rc, nz)
-    for o in range(1, 4):
-        other = lax.rem(col + o, 4)
-        arrived(qg, other, q_recv.at[other])
-    for r in range(4):
-        xpq_ref[0, r] = xg[2 + r, 0:48, :]
-        xpq_ref[1, r] = pg[2 + r]
-        xpq_ref[2, r] = qg[r]
+    gram_out = pltpu.make_async_copy(z_ref, z_hbm, out_sem.at[0])
+    gram_out.start()
     for copy in sent:
         copy.wait_send()
     for x in range(4):
@@ -364,6 +383,9 @@
         def _():
             to_line(x).wait_send()
     halo.wait_send()
+    gram_out.wait()
+    for copy in products_out:
+        copy.wait()
 
 
 def per_device(ny, nz, positions, trial_block, pair_tiles, pair_count):
@@ -371,16 +393,19 @@
     vmem = pl.BlockSpec(memory_space=pltpu.VMEM)
     dma = pltpu.SemaphoreType.DMA
     hbm = pl.BlockSpec(memory_space=pltpu.HBM)
+    block = trial_block.reshape(48, 512)
     products, gram = pl.pallas_call(
         functools.partial(kernel, ny, nz),
-        out_shape=(jax.ShapeDtypeStruct((3, 4, 48, 128), F32), jax.ShapeDtypeStruct((16, 128), F32)),
+        out_shape=(jax.ShapeDtypeStruct((2, 4, 48, 128), F32), jax.ShapeDtypeStruct((16, 128), F32)),
         in_specs=[hbm] * 4,
-        out_specs=(vmem, vmem),
+        out_specs=(hbm, hbm),
         scratch_shapes=[
             pltpu.VMEM((3, 512), F32),
             pltpu.VMEM((2, 4, 8), jnp.int32),
             pltpu.VMEM((1, 4), jnp.int32),
             dma((7,)),
+            pltpu.VMEM((16, 128), F32),
+            dma((3,)),
             pltpu.VMEM((8, 56, 128), F32),
             pltpu.VMEM((8, 48, 128), F32),
             pltpu.VMEM((4, 48, 128), F32),
@@ -399,9 +424,9 @@
             dma((ny,)), dma((ny,)),
             dma((2, nz)), dma((nz,)),
         ],
-        compiler_params=pltpu.CompilerParams(collective_id=0, has_side_effects=True, vmem_limit_bytes=16 << 20),
+        compiler_params=pltpu.CompilerParams(collective_id=0, has_side_effects=True, vmem_limit_bytes=60 * 1024 * 1024),
         name="gram_blocks",
-    )(trial_block.reshape(48, 512), positions, pair_tiles.reshape(2, 4, 8), pair_count)
+    )(block, positions, pair_tiles.reshape(2, 4, 8), pair_count)
     block, rayleigh, correlation, norms = pl.pallas_call(
         functools.partial(finish, scale),
         out_shape=(
@@ -410,11 +435,12 @@
             jax.ShapeDtypeStruct((16, 16), F32),
             jax.ShapeDtypeStruct((1, 16), F32),
         ),
-        in_specs=[vmem] * 2,
+        in_specs=[hbm] * 3,
         out_specs=(vmem,) * 4,
-        compiler_params=pltpu.CompilerParams(vmem_limit_bytes=16 << 20),
+        scratch_shapes=[pltpu.VMEM((48, 512), F32), pltpu.VMEM((2, 4, 48, 128), F32), pltpu.VMEM((16, 128), F32), dma((3,))],
+        compiler_params=pltpu.CompilerParams(vmem_limit_bytes=60 * 1024 * 1024),
         name="finish",
-    )(products, gram)
+    )(block, products, gram)
     return block.reshape(3, 16, 512), rayleigh, correlation, norms.reshape(16)
 
 

time: 44 us -> 40.4 us (0.918)
  local copies, waits for them, and re-layouts: 2.92 us -> 0 us
  Pallas kernels: 40.2 us -> 39.6 us
    unnamed x8 -> x0, local copies, waits for them, and re-layouts: 2.92 us -> none
    pallas_call x1, Pallas kernels: 4.03 us -> 2.85 us  [per_device(): pl.pallas_call(functools.partial(finish, scale), out_shape=(jax.ShapeDtyp...]
    pallas_call x1, Pallas kernels: 36.2 us -> 36.8 us  [per_device(): pl.pallas_call(functools.partial(kernel, ny, nz), out_shape=(jax.ShapeDty...]
where the time goes in v2:
time: 40.4 us; the launch traced here: 40.2 us
  Pallas kernels  39.6 us (98%)
  between operations  0.64 us (2%)
    pallas_call x1, Pallas kernels, per_device(): pl.pallas_call(functools.partial(kernel, ny, nz), out_shape=(jax.ShapeDty...  36.8 us
    pallas_call x1, Pallas kernels, per_device(): pl.pallas_call(functools.partial(finish, scale), out_shape=(jax.ShapeDtyp...  2.85 us

profile of v2, /device:TPU:1, one launch (start us, length us, event | category | flops | bytes accessed | tf_op | source)
XLA Modules:
  0.0 40.2 jit_solution(1330654483514921973)
XLA Ops:
  0.6 36.8 %gram_blocks.1 = (f32[2,4,48,128]{3,2,1,0:T(8,128)}, f32[16,128]{1,0:T(8,128)}) custom-call(f32[48,512]{1,0:T(8,128)} %bitcast.4, f32[3,512]{1,0:T(4,128)} %pos_hbm.1, s32[2,4,8]{2,1,0:T(4,128)} %bitcast.6, s32[1,4]{1,0:T(1,128)} %count_hbm.1), custom_call_target="tpu_custom_call" | custom-call | tf_op jit(solution)/shard_map/gram_blocks/pallas_call | solution.py:397
  37.4 2.8 %finish.1 = (f32[48,512]{1,0:T(8,128)}, f32[16,16]{1,0:T(8,128)}, f32[16,16]{1,0:T(8,128)}, f32[1,16]{1,0:T(1,128)}) custom-call(f32[48,512]{1,0:T(8,128)} %bitcast.5, f32[2,4,48,128]{3,2,1,0:T(8,128)} %get-tuple-element.10.pq_hbm, f32[16,128]{1,0:T(8,128)} %get-tuple-element.11.z_hbm), custom_call_target="tpu_custom_call" | custom-call | tf_op jit(solution)/shard_map/finish/pallas_call | solution.py:430

commit v3 on v2

--- a/solution.py
+++ b/solution.py
@@ -57,9 +57,14 @@
     for copy in (gram_in, x_in, pq_in):
         copy.start()
     gram_in.wait()
-    xx, xp, pp, pq = (z_ref[:, 16 * i : 16 * i + 16] for i in range(4))
-    qq = z_ref[:, 64:65]
-    eye = iota((16, 16), 0) == iota((16, 16), 1)
+    packed = jnp.concatenate([z_ref[:, 0:64], z_ref[:, 64:128]], axis=0)
+    xp, pq, mix = (packed[:, 16 * i : 16 * i + 16] for i in range(3))
+    qq = packed[:, 49:50]
+    flipped = jnp.transpose(mix)
+    row, col = iota((16, 16), 0), iota((16, 16), 1)
+    eye = row == col
+    xx = jnp.where(col <= row, mix, flipped)
+    pp = jnp.where(eye, packed[:, 48:49], jnp.where(col > row, mix, flipped))
     one = jnp.where(eye, 1.0, 0.0).astype(F32)
     c0 = solve(xx, xp)
     at = one + STEP * c0
@@ -169,6 +174,7 @@
         xg[2 + r, 51:52, :] = listed
 
     dacc[...] = jnp.zeros_like(dacc)
+    pay[...] = jnp.zeros_like(pay)
     own = 2 + col
 
     def spring_block(q, slot):
@@ -264,28 +270,55 @@
     here, first_product = finish_product(gathered, xg)
     for d in range(3):
         pg[own, d * 16 : (d + 1) * 16, :] = first_product[d]
-    sent = []
-    for n, c in enumerate(across_cols):
-        sent.append(
-            pltpu.make_async_remote_copy(
-                src_ref=pg.at[own], dst_ref=pg.at[jnp.where(low, 6 + col, col - 2)], send_sem=p_send.at[n],
-                recv_sem=p_recv.at[jnp.where(low, 6 + col, col - 2)], device_id=at_tile(across, c), device_id_type=MESH,
-            )
+    edge = jnp.logical_or(col == 0, col == 3)
+
+    def across_copy(n, c):
+        slot = jnp.where(low, 6 + col, col - 2)
+        return pltpu.make_async_remote_copy(
+            src_ref=pg.at[own], dst_ref=pg.at[slot], send_sem=p_send.at[n], recv_sem=p_recv.at[slot],
+            device_id=at_tile(across, c), device_id_type=MESH,
         )
-    for o in range(1, 4):
-        sent.append(moved(pg, own, p_send.at[1 + o], p_recv.at[own], (ty, tz, core, lax.rem(col + o, 4))))
-    for copy in sent:
-        copy.start()
+
+    def line_copy(o):
+        return moved(pg, own, p_send.at[1 + o], p_recv.at[own], (ty, tz, core, lax.rem(col + o, 4)))
+
+    def rest_copy(o):
+        return moved(qg, col, q_send.at[o - 1], q_recv.at[col], (ty, tz, core, lax.rem(col + o, 4)))
+
+    near_across = across_copy(0, jnp.where(low, 3, 0))
+    next_across = across_copy(1, jnp.where(low, 2, 1))
+
+    def is_far(o):
+        return jnp.logical_and(edge, lax.rem(col + o, 4) == 3 - col)
+
+    near_across.start()
+
+    @pl.when(edge)
+    def _():
+        next_across.start()
+
+    for o in (2, 1, 3):
+        @pl.when(jnp.logical_not(is_far(o)))
+        def _():
+            line_copy(o).start()
 
     def arrived(buf, slot, recv):
         moved(buf, slot, p_send.at[0], recv, (ty, tz, core, lax.rem(col + 1, 4))).wait_recv()
 
     for o in range(1, 4):
         other = 2 + lax.rem(col + o, 4)
-        arrived(pg, other, p_recv.at[other])
-    for n in range(2):
-        other = jnp.where(low, n, 6 + n)
-        arrived(pg, other, p_recv.at[other])
+
+        @pl.when(jnp.logical_not(is_far(o)))
+        def _():
+            arrived(pg, other, p_recv.at[other])
+
+    near_slot = jnp.where(low, 1, 6)
+    arrived(pg, near_slot, p_recv.at[near_slot])
+
+    @pl.when(edge)
+    def _():
+        next_slot = jnp.where(low, 0, 7)
+        arrived(pg, next_slot, p_recv.at[next_slot])
 
     for q in range(5):
         near_vectors(pg, q)
@@ -294,10 +327,17 @@
     for d in range(3):
         qg[col, d * 16 : (d + 1) * 16, :] = second_product[d]
     x, p, q = (jnp.concatenate(parts, axis=1) for parts in (here, first_product, second_product))
-    z = mm_exact(jnp.concatenate([x, p], axis=0), jnp.concatenate([x, p, q], axis=0), transposed=True)
-    pay[:, 0:32] = z[0:16, 0:32]
-    pay[:, 32:64] = z[16:32, 16:48]
-    pay[:, 64:128] = jnp.broadcast_to(jnp.sum(q * q, axis=1, keepdims=True), (16, 64))
+    z_x = mm_exact(jnp.concatenate([x, p], axis=0), x, transposed=True)
+    z_p = mm_exact(p, jnp.concatenate([p, q], axis=0), transposed=True)
+    mix = jnp.where(iota((16, 16), 1) <= iota((16, 16), 0), z_x[0:16], z_p[:, 0:16])
+    p_sq, q_sq = (jnp.sum(v * v, axis=1, keepdims=True) for v in (p, q))
+    for h in range(2):
+        rows, at = slice(8 * h, 8 * h + 8), 64 * h
+        pay[:, at : at + 16] = z_x[16:32][rows]
+        pay[:, at + 16 : at + 32] = z_p[rows, 16:32]
+        pay[:, at + 32 : at + 48] = mix[rows]
+        pay[:, at + 48 : at + 49] = p_sq[rows]
+        pay[:, at + 49 : at + 50] = q_sq[rows]
 
     line = col * 2 + core
 
@@ -312,11 +352,6 @@
         def _():
             to_line(x).start()
 
-    for o in range(1, 4):
-        copy = moved(qg, col, q_send.at[o - 1], q_recv.at[col], (ty, tz, core, lax.rem(col + o, 4)))
-        copy.start()
-        sent.append(copy)
-
     def summed(buf, n):
         parts = [buf[i] for i in range(n)]
         while len(parts) > 1:
@@ -333,8 +368,20 @@
 
     def put_products():
         for o in range(1, 4):
+            rest_copy(o).start()
+
+            @pl.when(is_far(o))
+            def _():
+                line_copy(o).start()
+
+        for o in range(1, 4):
             other = lax.rem(col + o, 4)
             arrived(qg, other, q_recv.at[other])
+
+            @pl.when(is_far(o))
+            def _():
+                arrived(pg, 2 + other, p_recv.at[2 + other])
+
         for copy in products_out:
             copy.start()
 
@@ -366,9 +413,15 @@
             moved(rc, other, c_send.at[0, 0], c_recv.at[other], (ty, tz, 0, col)).wait_recv()
         for copy in done:
             copy.wait_send()
+        for x in range(4):
+            @pl.when(col != x)
+            def _():
+                to_line(x).wait_send()
 
     @pl.when(core == 0)
     def _():
+        for x in range(4):
+            to_line(x).wait_send()
         put_products()
         for other in range(nz):
             moved(rc, other, c_send.at[0, 0], c_recv.at[other], (ty, tz, 1, col)).wait_recv()
@@ -376,12 +429,15 @@
     z_ref[...] = summed(rc, nz)
     gram_out = pltpu.make_async_copy(z_ref, z_hbm, out_sem.at[0])
     gram_out.start()
-    for copy in sent:
-        copy.wait_send()
-    for x in range(4):
-        @pl.when(jnp.logical_or(core == 0, col != x))
-        def _():
-            to_line(x).wait_send()
+    near_across.wait_send()
+
+    @pl.when(edge)
+    def _():
+        next_across.wait_send()
+
+    for o in range(1, 4):
+        line_copy(o).wait_send()
+        rest_copy(o).wait_send()
     halo.wait_send()
     gram_out.wait()
     for copy in products_out:
@@ -396,7 +452,7 @@
     block = trial_block.reshape(48, 512)
     products, gram = pl.pallas_call(
         functools.partial(kernel, ny, nz),
-        out_shape=(jax.ShapeDtypeStruct((2, 4, 48, 128), F32), jax.ShapeDtypeStruct((16, 128), F32)),
+        out_shape=(jax.ShapeDtypeStruct((2, 4, 48, 128), F32), jax.ShapeDtypeStruct((8, 128), F32)),
         in_specs=[hbm] * 4,
         out_specs=(hbm, hbm),
         scratch_shapes=[
@@ -404,7 +460,7 @@
             pltpu.VMEM((2, 4, 8), jnp.int32),
             pltpu.VMEM((1, 4), jnp.int32),
             dma((7,)),
-            pltpu.VMEM((16, 128), F32),
+            pltpu.VMEM((8, 128), F32),
             dma((3,)),
             pltpu.VMEM((8, 56, 128), F32),
             pltpu.VMEM((8, 48, 128), F32),
@@ -413,10 +469,10 @@
             pltpu.VMEM((640, 768), BF16),
             pltpu.VMEM((96, 640), BF16),
             pltpu.VMEM((6, 8, 128), F32),
-            pltpu.VMEM((16, 128), F32),
-            pltpu.VMEM((8, 16, 128), F32),
-            pltpu.VMEM((ny, 16, 128), F32),
-            pltpu.VMEM((nz, 16, 128), F32),
+            pltpu.VMEM((8, 128), F32),
+            pltpu.VMEM((8, 8, 128), F32),
+            pltpu.VMEM((ny, 8, 128), F32),
+            pltpu.VMEM((nz, 8, 128), F32),
             dma, dma,
             dma((5,)), dma((8,)),
             dma((3,)), dma((4,)),
@@ -437,7 +493,7 @@
         ),
         in_specs=[hbm] * 3,
         out_specs=(vmem,) * 4,
-        scratch_shapes=[pltpu.VMEM((48, 512), F32), pltpu.VMEM((2, 4, 48, 128), F32), pltpu.VMEM((16, 128), F32), dma((3,))],
+        scratch_shapes=[pltpu.VMEM((48, 512), F32), pltpu.VMEM((2, 4, 48, 128), F32), pltpu.VMEM((8, 128), F32), dma((3,))],
         compiler_params=pltpu.CompilerParams(vmem_limit_bytes=60 * 1024 * 1024),
         name="finish",
     )(block, products, gram)

time: 40.4 us -> 40.3 us (level)
  no operation moved by 1% of the time
where the time goes in v3:
time: 40.3 us; the launch traced here: 40.1 us
  Pallas kernels  39.4 us (98%)
  between operations  0.64 us (2%)
    pallas_call x1, Pallas kernels, per_device(): pl.pallas_call(functools.partial(kernel, ny, nz), out_shape=(jax.ShapeDty...  36.4 us
    pallas_call x1, Pallas kernels, per_device(): pl.pallas_call(functools.partial(finish, scale), out_shape=(jax.ShapeDtyp...  3.03 us

profile of v3, /device:TPU:1, one launch (start us, length us, event | category | flops | bytes accessed | tf_op | source)
XLA Modules:
  0.0 40.1 jit_solution(7759941110187196662)
XLA Ops:
  0.6 36.4 %gram_blocks.1 = (f32[2,4,48,128]{3,2,1,0:T(8,128)}, f32[8,128]{1,0:T(8,128)}) custom-call(f32[48,512]{1,0:T(8,128)} %bitcast.4, f32[3,512]{1,0:T(4,128)} %pos_hbm.1, s32[2,4,8]{2,1,0:T(4,128)} %bitcast.6, s32[1,4]{1,0:T(1,128)} %count_hbm.1), custom_call_target="tpu_custom_call" | custom-call | tf_op jit(solution)/shard_map/gram_blocks/pallas_call | solution.py:453
  37.0 3.0 %finish.1 = (f32[48,512]{1,0:T(8,128)}, f32[16,16]{1,0:T(8,128)}, f32[16,16]{1,0:T(8,128)}, f32[1,16]{1,0:T(1,128)}) custom-call(f32[48,512]{1,0:T(8,128)} %bitcast.5, f32[2,4,48,128]{3,2,1,0:T(8,128)} %get-tuple-element.10.pq_hbm, f32[8,128]{1,0:T(8,128)} %get-tuple-element.11.z_hbm), custom_call_target="tpu_custom_call" | custom-call | tf_op jit(solution)/shard_map/finish/pallas_call | solution.py:486

commit v4 on v3

--- a/solution.py
+++ b/solution.py
@@ -102,7 +102,7 @@
     pq_hbm, z_hbm,
     pos_ref, pairs_ref, count_ref, in_sem, z_ref, out_sem,
     xg, pg, qg, shi, slo, lw, dacc, pay, ra, rb, rc,
-    halo_send, halo_recv, p_send, p_recv, q_send, q_recv, a_send, a_recv, b_send, b_recv, c_send, c_recv,
+    halo_send, halo_recv, p_send, p_recv, far_send, far_recv, q_send, q_recv, a_send, a_recv, b_send, b_recv, c_send, c_recv,
 ):
     ty, tz, core, col = (lax.axis_index(n) for n in ("ty", "tz", "core", "col"))
     tiles = ny * nz * 2
@@ -123,7 +123,7 @@
     ]
     for r in range(4):
         lanes = slice(r * 128, (r + 1) * 128)
-        fetches.append(pltpu.make_async_copy(x_hbm.at[:, lanes], xg.at[2 + r, 0:48, :], in_sem.at[3 + r]))
+        fetches.append(pltpu.make_async_copy(x_hbm.at[:, lanes], xg.at[2 + r, 0:48, :], in_sem.at[3]))
     for fetch in fetches:
         fetch.start()
 
@@ -153,8 +153,9 @@
         greet((ty, tz, 1 - core, lax.rem(col + o, 4)))
     greet((ty, tz, 1 - core, col))
 
-    for fetch in fetches:
+    for fetch in fetches[:3]:
         fetch.wait()
+    pltpu.make_async_copy(xg.at[2:6, 0:48, :], xg.at[2:6, 0:48, :], in_sem.at[3]).wait()
     lane = iota((1, 128), 1)
     rows, cols = pairs_ref[0], pairs_ref[1]
     slot_col = iota((4, 8), 0)
@@ -210,15 +211,20 @@
 
     pl.semaphore_wait(barrier, 11 + core * (ny + 2 * nz - 3))
     from_slot, to_slot = jnp.where(low, 4, 2), jnp.where(low, 0, 6)
-    halo = pltpu.make_async_remote_copy(
-        src_ref=xg.at[pl.ds(from_slot, 2)],
-        dst_ref=xg.at[pl.ds(to_slot, 2)],
-        send_sem=halo_send,
-        recv_sem=halo_recv,
-        device_id=at_tile(jnp.where(low, after, before), col),
-        device_id_type=MESH,
-    )
-    halo.start()
+
+    def halo_copy(n, rows):
+        return pltpu.make_async_remote_copy(
+            src_ref=xg.at[pl.ds(from_slot, 2), rows],
+            dst_ref=xg.at[pl.ds(to_slot, 2), rows],
+            send_sem=halo_send.at[n],
+            recv_sem=halo_recv.at[n],
+            device_id=at_tile(jnp.where(low, after, before), col),
+            device_id_type=MESH,
+        )
+
+    halo = (halo_copy(0, slice(48, 56)), halo_copy(1, slice(0, 48)))
+    for copy in halo:
+        copy.start()
 
     def near_vectors(source, q):
         hi, lo = split(source[slots[q], 0:48, :])
@@ -238,13 +244,14 @@
     for q in range(3):
         near_vectors(xg, q)
     gathered = near_sum(0, 3)
-    halo.wait_recv()
+    halo[0].wait_recv()
 
     def late_blocks(q, carry):
         spring_block(3 + q, jnp.where(q == 0, late[0], late[1]))
         return carry
 
     lax.fori_loop(0, 2, late_blocks, 0)
+    halo[1].wait_recv()
     for q in range(3, 5):
         near_vectors(xg, q)
     gathered = gathered + near_sum(3, 5)
@@ -262,6 +269,12 @@
             out.append(acc)
         return here, out
 
+    def all_sent(buf, send):
+        moved(buf, slice(None), send, q_recv, (ty, tz, 1 - core, col)).wait_send()
+
+    def all_here(buf, recv):
+        moved(buf, slice(None), q_send, recv, (ty, tz, 1 - core, col)).wait_recv()
+
     def moved(buf, at, send, recv, where):
         return pltpu.make_async_remote_copy(
             src_ref=buf.at[at], dst_ref=buf.at[at], send_sem=send, recv_sem=recv, device_id=where, device_id_type=MESH
@@ -272,21 +285,21 @@
         pg[own, d * 16 : (d + 1) * 16, :] = first_product[d]
     edge = jnp.logical_or(col == 0, col == 3)
 
-    def across_copy(n, c):
+    def across_copy(c):
         slot = jnp.where(low, 6 + col, col - 2)
         return pltpu.make_async_remote_copy(
-            src_ref=pg.at[own], dst_ref=pg.at[slot], send_sem=p_send.at[n], recv_sem=p_recv.at[slot],
+            src_ref=pg.at[own], dst_ref=pg.at[slot], send_sem=p_send, recv_sem=p_recv,
             device_id=at_tile(across, c), device_id_type=MESH,
         )
 
-    def line_copy(o):
-        return moved(pg, own, p_send.at[1 + o], p_recv.at[own], (ty, tz, core, lax.rem(col + o, 4)))
+    def line_copy(o, send, recv):
+        return moved(pg, own, send, recv, (ty, tz, core, lax.rem(col + o, 4)))
 
     def rest_copy(o):
-        return moved(qg, col, q_send.at[o - 1], q_recv.at[col], (ty, tz, core, lax.rem(col + o, 4)))
-
-    near_across = across_copy(0, jnp.where(low, 3, 0))
-    next_across = across_copy(1, jnp.where(low, 2, 1))
+        return moved(qg, col, q_send, q_recv, (ty, tz, core, lax.rem(col + o, 4)))
+
+    near_across = across_copy(jnp.where(low, 3, 0))
+    next_across = across_copy(jnp.where(low, 2, 1))
 
     def is_far(o):
         return jnp.logical_and(edge, lax.rem(col + o, 4) == 3 - col)
@@ -300,25 +313,9 @@
     for o in (2, 1, 3):
         @pl.when(jnp.logical_not(is_far(o)))
         def _():
-            line_copy(o).start()
-
-    def arrived(buf, slot, recv):
-        moved(buf, slot, p_send.at[0], recv, (ty, tz, core, lax.rem(col + 1, 4))).wait_recv()
-
-    for o in range(1, 4):
-        other = 2 + lax.rem(col + o, 4)
-
-        @pl.when(jnp.logical_not(is_far(o)))
-        def _():
-            arrived(pg, other, p_recv.at[other])
-
-    near_slot = jnp.where(low, 1, 6)
-    arrived(pg, near_slot, p_recv.at[near_slot])
-
-    @pl.when(edge)
-    def _():
-        next_slot = jnp.where(low, 0, 7)
-        arrived(pg, next_slot, p_recv.at[next_slot])
+            line_copy(o, p_send, p_recv).start()
+
+    all_here(pg.at[0:4], p_recv)
 
     for q in range(5):
         near_vectors(pg, q)
@@ -343,7 +340,7 @@
 
     def to_line(x):
         return pltpu.make_async_remote_copy(
-            src_ref=pay, dst_ref=ra.at[line], send_sem=a_send.at[x], recv_sem=a_recv.at[line],
+            src_ref=pay, dst_ref=ra.at[line], send_sem=a_send, recv_sem=a_recv,
             device_id=(ty, tz, 1, x), device_id_type=MESH,
         )
 
@@ -351,6 +348,12 @@
         @pl.when(jnp.logical_or(core == 0, col != x))
         def _():
             to_line(x).start()
+
+    def y_copy(o):
+        return moved(rb, ty, b_send, b_recv, (lax.rem(ty + o, ny), tz, 1, col))
+
+    def z_copy(o, c):
+        return moved(rc, tz, c_send.at[c], c_recv, (ty, lax.rem(tz + o, nz), c, col))
 
     def summed(buf, n):
         parts = [buf[i] for i in range(n)]
@@ -372,15 +375,13 @@
 
             @pl.when(is_far(o))
             def _():
-                line_copy(o).start()
-
-        for o in range(1, 4):
-            other = lax.rem(col + o, 4)
-            arrived(qg, other, q_recv.at[other])
-
-            @pl.when(is_far(o))
-            def _():
-                arrived(pg, 2 + other, p_recv.at[2 + other])
+                line_copy(o, far_send, far_recv).start()
+
+        all_here(qg.at[0:3], q_recv)
+
+        @pl.when(edge)
+        def _():
+            all_here(pg.at[0], far_recv)
 
         for copy in products_out:
             copy.start()
@@ -388,57 +389,45 @@
     @pl.when(core == 1)
     def _():
         ra[line] = pay[...]
-        for o in range(1, 8):
-            other = lax.rem(line + o, 8)
-            moved(ra, other, a_send.at[0], a_recv.at[other], (ty, tz, 0, col)).wait_recv()
+        all_here(ra.at[0:7], a_recv)
         rb[ty] = summed(ra, 8)
-        done = []
         for o in far_first(ny):
-            done.append(moved(rb, ty, b_send.at[o], b_recv.at[ty], (lax.rem(ty + o, ny), tz, 1, col)))
-            done[-1].start()
+            y_copy(o).start()
         put_products()
-        for o in range(1, ny):
-            other = lax.rem(ty + o, ny)
-            moved(rb, other, b_send.at[o], b_recv.at[other], (other, tz, 1, col)).wait_recv()
+        all_here(rb.at[0 : ny - 1], b_recv)
         rc[tz] = summed(rb, ny)
         for o in far_first(nz) + [0]:
-            place = lax.rem(tz + o, nz)
-            done.append(moved(rc, tz, c_send.at[0, o], c_recv.at[tz], (ty, place, 0, col)))
-            done[-1].start()
+            z_copy(o, 0).start()
             if o:
-                done.append(moved(rc, tz, c_send.at[1, o], c_recv.at[tz], (ty, place, 1, col)))
-                done[-1].start()
-        for o in range(1, nz):
-            other = lax.rem(tz + o, nz)
-            moved(rc, other, c_send.at[0, 0], c_recv.at[other], (ty, tz, 0, col)).wait_recv()
-        for copy in done:
-            copy.wait_send()
-        for x in range(4):
-            @pl.when(col != x)
-            def _():
-                to_line(x).wait_send()
+                z_copy(o, 1).start()
+        all_here(rc.at[0 : nz - 1], c_recv)
 
     @pl.when(core == 0)
     def _():
-        for x in range(4):
-            to_line(x).wait_send()
+        all_sent(ra.at[0:4], a_send)
         put_products()
-        for other in range(nz):
-            moved(rc, other, c_send.at[0, 0], c_recv.at[other], (ty, tz, 1, col)).wait_recv()
+        all_here(rc, c_recv)
 
     z_ref[...] = summed(rc, nz)
     gram_out = pltpu.make_async_copy(z_ref, z_hbm, out_sem.at[0])
     gram_out.start()
-    near_across.wait_send()
+
+    @pl.when(core == 1)
+    def _():
+        all_sent(ra.at[0:3], a_send)
+        all_sent(rb.at[0 : ny - 1], b_send)
+        all_sent(rc, c_send.at[0])
+        all_sent(rc.at[0 : nz - 1], c_send.at[1])
+
+    all_sent(pg.at[0:4], p_send)
+    all_sent(qg.at[0:3], q_send)
 
     @pl.when(edge)
     def _():
-        next_across.wait_send()
-
-    for o in range(1, 4):
-        line_copy(o).wait_send()
-        rest_copy(o).wait_send()
-    halo.wait_send()
+        all_sent(pg.at[0], far_send)
+
+    for copy in halo:
+        copy.wait_send()
     gram_out.wait()
     for copy in products_out:
         copy.wait()
@@ -459,7 +448,7 @@
             pltpu.VMEM((3, 512), F32),
             pltpu.VMEM((2, 4, 8), jnp.int32),
             pltpu.VMEM((1, 4), jnp.int32),
-            dma((7,)),
+            dma((4,)),
             pltpu.VMEM((8, 128), F32),
             dma((3,)),
             pltpu.VMEM((8, 56, 128), F32),
@@ -473,12 +462,9 @@
             pltpu.VMEM((8, 8, 128), F32),
             pltpu.VMEM((ny, 8, 128), F32),
             pltpu.VMEM((nz, 8, 128), F32),
-            dma, dma,
-            dma((5,)), dma((8,)),
-            dma((3,)), dma((4,)),
-            dma((4,)), dma((8,)),
-            dma((ny,)), dma((ny,)),
-            dma((2, nz)), dma((nz,)),
+            dma((2,)), dma((2,)),
+            dma, dma, dma, dma, dma, dma, dma, dma, dma, dma,
+            dma((2,)), dma,
         ],
         compiler_params=pltpu.CompilerParams(collective_id=0, has_side_effects=True, vmem_limit_bytes=60 * 1024 * 1024),
         name="gram_blocks",

time: 40.3 us -> 39 us (0.968)
  Pallas kernels: 39.4 us -> 38.2 us
    pallas_call x1, Pallas kernels: 36.4 us -> 35.2 us  [per_device(): pl.pallas_call(functools.partial(kernel, ny, nz), out_shape=(jax.ShapeDty...]
where the time goes in v4:
time: 39 us; the launch traced here: 38.8 us
  Pallas kernels  38.2 us (98%)
  between operations  0.64 us (2%)
    pallas_call x1, Pallas kernels, per_device(): pl.pallas_call(functools.partial(kernel, ny, nz), out_shape=(jax.ShapeDty...  35.2 us
    pallas_call x1, Pallas kernels, per_device(): pl.pallas_call(functools.partial(finish, scale), out_shape=(jax.ShapeDtyp...  3.03 us

profile of v4, /device:TPU:1, one launch (start us, length us, event | category | flops | bytes accessed | tf_op | source)
XLA Modules:
  0.0 38.8 jit_solution(7021082835432670579)
XLA Ops:
  0.6 35.2 %gram_blocks.1 = (f32[2,4,48,128]{3,2,1,0:T(8,128)}, f32[8,128]{1,0:T(8,128)}) custom-call(f32[48,512]{1,0:T(8,128)} %bitcast.4, f32[3,512]{1,0:T(4,128)} %pos_hbm.1, s32[2,4,8]{2,1,0:T(4,128)} %bitcast.6, s32[1,4]{1,0:T(1,128)} %count_hbm.1), custom_call_target="tpu_custom_call" | custom-call | tf_op jit(solution)/shard_map/gram_blocks/pallas_call | solution.py:442
  35.8 3.0 %finish.1 = (f32[48,512]{1,0:T(8,128)}, f32[16,16]{1,0:T(8,128)}, f32[16,16]{1,0:T(8,128)}, f32[1,16]{1,0:T(1,128)}) custom-call(f32[48,512]{1,0:T(8,128)} %bitcast.5, f32[2,4,48,128]{3,2,1,0:T(8,128)} %get-tuple-element.10.pq_hbm, f32[8,128]{1,0:T(8,128)} %get-tuple-element.11.z_hbm), custom_call_target="tpu_custom_call" | custom-call | tf_op jit(solution)/shard_map/finish/pallas_call | solution.py:472

commit v5 on v4

--- a/solution.py
+++ b/solution.py
@@ -315,6 +315,16 @@
         def _():
             line_copy(o, p_send, p_recv).start()
 
+    def pay_blocks(blocks):
+        for at, width, block in blocks:
+            for h in range(2):
+                pay[:, 64 * h + at : 64 * h + at + width] = block[8 * h : 8 * h + 8]
+
+    x, p = jnp.concatenate(here, axis=1), jnp.concatenate(first_product, axis=1)
+    z_x = mm_exact(jnp.concatenate([x, p], axis=0), x, transposed=True)
+    mix = jnp.where(iota((16, 16), 1) <= iota((16, 16), 0), z_x[0:16], mm_exact(p, p, transposed=True))
+    pay_blocks(((0, 16, z_x[16:32]), (32, 16, mix), (48, 1, jnp.sum(p * p, axis=1, keepdims=True))))
+
     all_here(pg.at[0:4], p_recv)
 
     for q in range(5):
@@ -323,18 +333,8 @@
 
     for d in range(3):
         qg[col, d * 16 : (d + 1) * 16, :] = second_product[d]
-    x, p, q = (jnp.concatenate(parts, axis=1) for parts in (here, first_product, second_product))
-    z_x = mm_exact(jnp.concatenate([x, p], axis=0), x, transposed=True)
-    z_p = mm_exact(p, jnp.concatenate([p, q], axis=0), transposed=True)
-    mix = jnp.where(iota((16, 16), 1) <= iota((16, 16), 0), z_x[0:16], z_p[:, 0:16])
-    p_sq, q_sq = (jnp.sum(v * v, axis=1, keepdims=True) for v in (p, q))
-    for h in range(2):
-        rows, at = slice(8 * h, 8 * h + 8), 64 * h
-        pay[:, at : at + 16] = z_x[16:32][rows]
-        pay[:, at + 16 : at + 32] = z_p[rows, 16:32]
-        pay[:, at + 32 : at + 48] = mix[rows]
-        pay[:, at + 48 : at + 49] = p_sq[rows]
-        pay[:, at + 49 : at + 50] = q_sq[rows]
+    q = jnp.concatenate(second_product, axis=1)
+    pay_blocks(((16, 16, mm_exact(p, q, transposed=True)), (49, 1, jnp.sum(q * q, axis=1, keepdims=True))))
 
     line = col * 2 + core
 

time: 39 us -> 39.1 us (level)
  no operation moved by 1% of the time
where the time goes in v5:
time: 39.1 us; the launch traced here: 38.9 us
  Pallas kernels  38.3 us (98%)
  between operations  0.64 us (2%)
    pallas_call x1, Pallas kernels, per_device(): pl.pallas_call(functools.partial(kernel, ny, nz), out_shape=(jax.ShapeDty...  35.3 us
    pallas_call x1, Pallas kernels, per_device(): pl.pallas_call(functools.partial(finish, scale), out_shape=(jax.ShapeDtyp...  3.03 us

profile of v5, /device:TPU:1, one launch (start us, length us, event | category | flops | bytes accessed | tf_op | source)
XLA Modules:
  0.0 38.9 jit_solution(7673998022675565840)
XLA Ops:
  0.6 35.3 %gram_blocks.1 = (f32[2,4,48,128]{3,2,1,0:T(8,128)}, f32[8,128]{1,0:T(8,128)}) custom-call(f32[48,512]{1,0:T(8,128)} %bitcast.4, f32[3,512]{1,0:T(4,128)} %pos_hbm.1, s32[2,4,8]{2,1,0:T(4,128)} %bitcast.6, s32[1,4]{1,0:T(1,128)} %count_hbm.1), custom_call_target="tpu_custom_call" | custom-call | tf_op jit(solution)/shard_map/gram_blocks/pallas_call | solution.py:442
  35.9 3.0 %finish.1 = (f32[48,512]{1,0:T(8,128)}, f32[16,16]{1,0:T(8,128)}, f32[16,16]{1,0:T(8,128)}, f32[1,16]{1,0:T(1,128)}) custom-call(f32[48,512]{1,0:T(8,128)} %bitcast.5, f32[2,4,48,128]{3,2,1,0:T(8,128)} %get-tuple-element.10.pq_hbm, f32[8,128]{1,0:T(8,128)} %get-tuple-element.11.z_hbm), custom_call_target="tpu_custom_call" | custom-call | tf_op jit(solution)/shard_map/finish/pallas_call | solution.py:472
